TPU v7x, 32 devices: a whole 2x2x4 slice. The times are simulated.
32 devices in a mesh: gx: 4 (over z), gy: 2 (over y), gz: 4 (over x, core).
Axes of the slice: x: 2, y: 2, z: 4, core: 2. Of those that a mesh axis runs over, the one named last changes fastest.
Arguments:
- cell_volume: float32 [64, 32, 512], P('gx', 'gy', 'gz'), may hold values from 0.5 to 2
- exponent: int32 [64, 32, 512], P('gx', 'gy', 'gz'), may hold values from 0 to 7
- owner_row: int32 [8192], P(('gx', 'gy', 'gz')), may hold values from 0 to 8191, as said below
Outputs:
- stencil_out: float32 [27, 8192, 128], P(None, ('gx', 'gy', 'gz'))
- lumped_out: float32 [8192, 128], P(('gx', 'gy', 'gz'))
Inputs may be any that keep to these rules, and one draw needn't show every extreme that they name: owner_row is a permutation of the row blocks; the row blocks of each device's share of owner_row go to each owner (owner_row // 256) exactly 8 times.
All inputs are finite; a program needn't handle non-finite values.
Results may differ from a plain program's by a relative error of at most 0.00007.
Values sent between devices are 32-bit elements; how exact they have to be, the bound alone decides.
A program may use at most 64 MiB of HBM per device.

v0:
```python
import jax
import jax.numpy as jnp
import numpy as np
from jax import lax
from jax.sharding import PartitionSpec as P

log_step = 0.3


def from_behind(block, axis, distance):
    devices = range(lax.axis_size(axis))
    route = [((i - distance) % len(devices), i) for i in devices]
    return lax.ppermute(block, axis, route)


def weight_table():
    table = np.zeros((27, 8), np.float32)
    for index_o in range(27):
        offsets = (index_o // 9 - 1, index_o // 3 % 3 - 1, index_o % 3 - 1)
        for index_a in range(8):
            corner = (index_a // 4, index_a // 2 % 2, index_a % 2)
            inside = all((0 <= corner[slot_d] + offsets[slot_d] <= 1 for slot_d in range(3)))
            factor = 1.0
            for slot_d in range(3):
                factor = factor * (2.0 if offsets[slot_d] == 0 else 1.0)
            table[index_o, index_a] = factor / 64.0 if inside else 0.0
    return table


def rim_section(current, along, stack_at, sender):
    length = current.shape[along]
    interior = lax.slice_in_dim(current, 0, length - 1, axis=along)
    top_layer = lax.slice_in_dim(current, length - 1, length, axis=along)
    received = sender(top_layer)
    behind = jnp.concatenate([received, interior], axis=along)
    return jnp.stack([current, behind], axis=stack_at)


def shards(cell_volume, exponent, owner_row):
    weight = cell_volume * jnp.exp(-log_step * exponent.astype(jnp.float32))
    span_x, span_y, span_z = weight.shape
    line_count = span_x * span_y
    devices_all = lax.axis_size(("gx", "gy", "gz"))

    def send_x(rim_layer):
        return from_behind(rim_layer, "gx", 1)

    def send_y(rim_layer):
        return from_behind(rim_layer, "gy", 1)

    owner_dev = owner_row // line_count
    by_owner = jnp.argsort(owner_dev, stable=True)
    slot_ids = (owner_row % line_count)[by_owner].reshape(1, devices_all, -1)
    table = jnp.asarray(weight_table())
    sectioned_x = rim_section(weight, 0, 0, send_x)
    sectioned_xy = rim_section(sectioned_x, 2, 1, send_y)
    lines = sectioned_xy.reshape(4, line_count, span_z)
    rim_values = from_behind(sectioned_xy[..., span_z - 1 :], "gz", 1).reshape(4, line_count)
    packed = lines[:, by_owner].reshape(4, devices_all, -1, span_z)
    rim_packed = rim_values[:, by_owner].reshape(4, devices_all, -1)
    got_lines, got_rims, got_slots = (
        lax.all_to_all(packed, ("gx", "gy", "gz"), split_axis=1, concat_axis=1, tiled=True),
        lax.all_to_all(rim_packed, ("gx", "gy", "gz"), split_axis=1, concat_axis=1, tiled=True),
        lax.all_to_all(slot_ids, ("gx", "gy", "gz"), split_axis=1, concat_axis=1, tiled=True),
    )
    placing = jnp.argsort(got_slots.reshape(-1))
    current = got_lines.reshape(4, line_count, span_z)[:, placing]
    before = got_rims.reshape(4, line_count)[:, placing]
    behind = jnp.concatenate([before[..., None], current[..., : span_z - 1]], axis=2)
    corners = jnp.stack([current, behind], axis=1).reshape(8, line_count, span_z)
    stencil_rows = jnp.einsum("oa,alz->olz", table, corners, precision=lax.Precision.HIGHEST)
    lumped_rows = 1.0 / jnp.sum(stencil_rows, axis=0)
    return (stencil_rows, lumped_rows)


def solution(mesh):
    return jax.shard_map(
        shards,
        mesh=mesh,
        in_specs=(P("gx", "gy", "gz"), P("gx", "gy", "gz"), P(("gx", "gy", "gz"))),
        out_specs=(P(None, ("gx", "gy", "gz"), None), P(("gx", "gy", "gz"), None)),
        check_vma=False,
    )
```

profile of v0, /device:TPU:0, one launch (start us, length us, event | category | flops | bytes accessed | tf_op | source)
XLA Modules:
  0.0 66.7 jit_solution(13630262406832950411)
XLA Ops:
  0.6 1.0 %exponential_multiply_fusion = f32[16,16,128]{2,1,0:T(8,128)S(1)} fusion(f32[16,16,128]{2,1,0:T(8,128)} %param.4, s32[16,16,128]{2,1,0:T(8,128)} %param.5), kind=kLoop, calls=%fused_computation.20 | loop fusion | flops 98304 | bytes 393216 | tf_op jit(solution)/shard_map/mul | solution.py:40
  1.6 3.1 %collective-permute-start = (f32[1,16,128]{2,1,0:T(8,128)S(1)}, f32[1,16,128]{2,1,0:T(8,128)S(1)}, u32[]{:S(2)}, u32[]{:S(2)}) collective-permute-start(f32[1,16,128]{2,1,0:T(8,128)S(1)} %slice.34), channel_id=1, source_target_pairs={{24,0},{0,8},{8,16},{16,24},{25,1},{1,9},{9,17},{17,25},{26,2},{2,... | collective-permute-start | bytes 24584 | tf_op jit(solution)/shard_map/ppermute | solution.py:13
  4.7 0.7 %and_select_fusion = (s32[256]{0:T(256)S(1)}, s32[256]{0:T(256)S(1)}) fusion(s32[256]{0:T(256)} %param.6), kind=kLoop, calls=%fused_computation.27 | loop fusion | flops 4864 | bytes 3072 | tf_op jit(solution)/shard_map/jit(remainder)/select_n | solution.py:53
  5.4 3.2 %sort.34 = (s32[256]{0:T(256)}, s32[256]{0:T(256)S(1)}) sort(s32[256]{0:T(256)S(1)} %get-tuple-element.15, s32[256]{0:T(256)S(1)} %iota.8), dimensions={0}, to_apply=%region_0.1 | sort | flops 2048 | bytes 4096 | tf_op jit(solution)/shard_map/jit(argsort)/sort | solution.py:52
  8.7 1.6 %collective-permute-start.1 = (f32[2,16,1,128]{3,2,1,0:T(1,128)S(1)}, f32[2,16,1,128]{3,2,1,0:T(1,128)S(1)}, u32[]{:S(2)}, u32[]{:S(2)}) collective-permute-start(f32[2,16,1,128]{3,2,1,0:T(1,128)S(1)} %fusion.3), channel_id=1, source_target_pairs={{4,0},{0,4},{5,1},{1,5},{6,2},{2,6},{7,3},{3,7},{12,8},{8,12},{13,... | collective-permute-start | bytes 49160 | tf_op jit(solution)/shard_map/ppermute | solution.py:13
  10.3 2.2 %collective-permute-done.1 = f32[2,16,1,128]{3,2,1,0:T(1,128)S(1)} collective-permute-done((f32[2,16,1,128]{3,2,1,0:T(1,128)S(1)}, f32[2,16,1,128]{3,2,1,0:T(1,128)S(1)}, u32[]{:S(2)}, u32[]{:S(2)}) %collective-permute-start.1) | collective-permute-done | bytes 16416 | tf_op jit(solution)/shard_map/ppermute | solution.py:13
  12.8 1.9 %gather_fusion.1 = s32[256]{0:T(256)S(1)} fusion(s32[256]{0:T(256)S(1)} %get-tuple-element.14, s32[1024]{0:T(1024)S(1)} %pad_clamp_fusion.1), kind=kCustom, calls=%fused_computation.1 | custom fusion | bytes 3072 | tf_op jit(solution)/shard_map/gather | solution.py:53
  14.8 0.7 %reshape.34 = s32[1,32,8]{2,1,0:T(8,128)} reshape(s32[256]{0:T(256)S(1)} %gather_fusion.1) | data formatting | bytes 2048 | tf_op jit(solution)/shard_map/reshape | solution.py:53
  15.5 5.1 %all-to-all-start.1 = ((s32[1,32,8]{2,0,1:T(1,128)}), s32[1,32,8]{2,0,1:T(1,128)S(1)}, u32[]{:S(2)}, u32[]{:S(2)}) async-start(s32[1,32,8]{2,0,1:T(1,128)} %bitcast.10), calls=%async_computation.1 | async-start | bytes 32768 | tf_op jit(solution)/shard_map/all_to_all | solution.py:64
  20.6 0.8 %collective-permute-done.2 = f32[2,2,16,16,1]{4,3,2,1,0:T(8,128)S(1)} collective-permute-done((f32[2,2,16,16,1]{4,3,2,1,0:T(8,128)S(1)}, f32[2,2,16,16,1]{4,3,2,1,0:T(8,128)S(1)}, u32[]{:S(2)}, u32[]{:S(2)}) %collective-permute-start.2) | collective-permute-done | bytes 4128 | tf_op jit(solution)/shard_map/ppermute | solution.py:13
  21.8 0.7 %gather_fusion.3 = f32[256,4]{1,0:T(8,128)S(1)} fusion(f32[4,256]{0,1:T(8,128)S(1)} %copy.25, s32[1024]{0:T(1024)S(1)} %pad_clamp_fusion.1), kind=kCustom, calls=%fused_computation.3 | custom fusion | bytes 9216 | tf_op jit(solution)/shard_map/gather | solution.py:60
  22.6 0.9 %copy.26 = f32[4,32,8]{2,0,1:T(4,128)} copy(f32[4,32,8]{0,2,1:T(8,128)S(1)} %bitcast.45) | data formatting | bytes 8192 | tf_op jit(solution)/shard_map/reshape | solution.py:60
  23.5 4.2 %all-to-all-done.1 = s32[1,32,8]{2,0,1:T(1,128)S(1)} async-done(((s32[1,32,8]{2,0,1:T(1,128)}), s32[1,32,8]{2,0,1:T(1,128)S(1)}, u32[]{:S(2)}, u32[]{:S(2)}) %all-to-all-start.1) | async-done | bytes 1056 | tf_op jit(solution)/shard_map/all_to_all | solution.py:64
  27.7 2.6 %all-to-all-start.2 = ((f32[4,32,8]{2,0,1:T(4,128)}), f32[4,32,8]{2,0,1:T(4,128)S(1)}, u32[]{:S(2)}, u32[]{:S(2)}) async-start(f32[4,32,8]{2,0,1:T(4,128)} %copy.26), calls=%async_computation.2 | async-start | bytes 131072 | tf_op jit(solution)/shard_map/all_to_all | solution.py:63
  30.3 0.3 copy.23
  30.7 1.8 %gather_fusion = f32[256,4,128]{2,1,0:T(4,128)} fusion(f32[4,256,128]{2,0,1:T(4,128)S(1)} %copy.23, s32[1024]{0:T(1024)S(1)} %pad_clamp_fusion.1), kind=kCustom, calls=%fused_computation | custom fusion | bytes 1049600 | tf_op jit(solution)/shard_map/gather | solution.py:59
  32.4 5.3 %all-to-all-done.2 = f32[4,32,8]{2,0,1:T(4,128)S(1)} async-done(((f32[4,32,8]{2,0,1:T(4,128)}), f32[4,32,8]{2,0,1:T(4,128)S(1)}, u32[]{:S(2)}, u32[]{:S(2)}) %all-to-all-start.2) | async-done | bytes 4128 | tf_op jit(solution)/shard_map/all_to_all | solution.py:63
  37.7 2.9 %all-to-all-start = ((f32[4,32,8,128]{3,0,2,1:T(4,128)}), f32[4,32,8,128]{3,0,2,1:T(4,128)S(1)}, u32[]{:S(2)}, u32[]{:S(2)}) async-start(f32[4,32,8,128]{3,0,2,1:T(4,128)} %bitcast.8), calls=%async_computation | async-start | bytes 1048576 | tf_op jit(solution)/shard_map/all_to_all | solution.py:62
  40.6 0.5 broadcast.55
  41.1 0.7 %reduce.4 = s32[32,8]{1,0:T(8,128)S(1)} reduce(s32[1,32,8]{2,0,1:T(1,128)S(1)} %all-to-all-done.1, s32[]{:T(128)} %broadcast.55), dimensions={0}, to_apply=%all_to_all.10.reduce_sub_computation.3 | reduce | bytes 2052 | tf_op jit(solution)/shard_map/all_to_all | solution.py:64
  41.9 3.2 %sort.35 = (s32[256]{0:T(256)}, s32[256]{0:T(256)S(1)}) sort(s32[256]{0:T(256)S(1)} %reshape.35, s32[256]{0:T(256)S(1)} %iota.9), dimensions={0}, to_apply=%region_1.2 | sort | flops 2048 | bytes 4096 | tf_op jit(solution)/shard_map/jit(argsort)/sort | solution.py:66
  45.1 0.3 copy.27
  45.3 0.7 %gather_fusion.4 = f32[256,4]{1,0:T(8,128)S(1)} fusion(f32[4,256]{0,1:T(8,128)S(1)} %bitcast.43, s32[1024]{0:T(1024)S(1)} %pad_clamp_fusion), kind=kCustom, calls=%fused_computation.4 | custom fusion | bytes 9216 | tf_op jit(solution)/shard_map/gather | solution.py:68
  46.1 1.7 %copy.29 = f32[4,256,1]{2,0,1:T(4,128)S(1)} copy(f32[4,256,1]{0,1,2:T(8,128)S(1)} %bitcast.44) | data formatting | bytes 8192 | tf_op jit(solution)/shard_map/broadcast_in_dim | solution.py:69
  47.7 8.3 %all-to-all-done = f32[4,32,8,128]{3,0,2,1:T(4,128)S(1)} async-done(((f32[4,32,8,128]{3,0,2,1:T(4,128)}), f32[4,32,8,128]{3,0,2,1:T(4,128)S(1)}, u32[]{:S(2)}, u32[]{:S(2)}) %all-to-all-start) | async-done | bytes 524320 | tf_op jit(solution)/shard_map/all_to_all | solution.py:62
  56.0 1.0 %gather_fusion.2 = f32[256,4,128]{2,1,0:T(4,128)S(1)} fusion(f32[4,256,128]{2,0,1:T(4,128)S(1)} %bitcast.41, s32[1024]{0:T(1024)S(1)} %pad_clamp_fusion), kind=kCustom, calls=%fused_computation.2 | custom fusion | bytes 1049600 | tf_op jit(solution)/shard_map/gather | solution.py:67
  57.0 0.3 maximum_bitcast_fusion
  57.4 0.2 pad_maximum_fusion
  57.6 0.8 %copy.30 = f32[4,2,256,128]{3,1,0,2:T(2,128)S(1)} copy(f32[4,2,256,128]{3,0,2,1:T(4,128)S(1)} %pad_maximum_fusion) | data formatting | bytes 2097152 | tf_op jit(solution)/shard_map/stack | solution.py:70
  58.4 3.7 %fusion.4 = (f32[256,128]{1,0:T(8,128)S(1)}, f32[27,256,128]{2,0,1:T(8,128)S(1)}) fusion(f32[27,8,1]{0,1,2:T(8,128)S(1)} %copy-done, f32[8,256,128]{2,0,1:T(8,128)S(1)} %bitcast.37), kind=kOutput, calls=%fused_computation.34 | convolution fusion | flops 85786624 | bytes 4719456 | tf_op jit(solution)/shard_map/oa,alz->olz/dot_general | solution.py:71
  62.2 0.7 %broadcast_divide_fusion = f32[256,128]{1,0:T(8,128)} fusion(f32[256,128]{1,0:T(8,128)S(1)} %get-tuple-element.16), kind=kLoop, calls=%fused_computation.21 | loop fusion | flops 32768 | bytes 262144 | tf_op jit(solution)/shard_map/div | solution.py:72
  62.8 3.8 %copy.31 = f32[27,256,128]{2,1,0:T(8,128)} copy(f32[27,256,128]{2,0,1:T(8,128)S(1)} %get-tuple-element.17) | data formatting | bytes 7077888
  (23 shorter events, 1.0 us)
Async XLA Ops:
  1.6 7.0 %collective-permute-start = (f32[1,16,128]{2,1,0:T(8,128)S(1)}, f32[1,16,128]{2,1,0:T(8,128)S(1)}, u32[]{:S(2)}, u32[]{:S(2)}) collective-permute-start(f32[1,16,128]{2,1,0:T(8,128)S(1)} %slice.34), channel_id=1, source_target_pairs={{24,0},{0,8},{8,16},{16,24},{25,1},{1,9},{9,17},{17,25},{26,2},{2,... | collective-permute-start | bytes 24584 | tf_op jit(solution)/shard_map/ppermute | solution.py:13
  8.7 3.8 %collective-permute-start.1 = (f32[2,16,1,128]{3,2,1,0:T(1,128)S(1)}, f32[2,16,1,128]{3,2,1,0:T(1,128)S(1)}, u32[]{:S(2)}, u32[]{:S(2)}) collective-permute-start(f32[2,16,1,128]{3,2,1,0:T(1,128)S(1)} %fusion.3), channel_id=1, source_target_pairs={{4,0},{0,4},{5,1},{1,5},{6,2},{2,6},{7,3},{3,7},{12,8},{8,12},{13,... | collective-permute-start | bytes 49160 | tf_op jit(solution)/shard_map/ppermute | solution.py:13
  12.7 8.7 %collective-permute-start.2 = (f32[2,2,16,16,1]{4,3,2,1,0:T(8,128)S(1)}, f32[2,2,16,16,1]{4,3,2,1,0:T(8,128)S(1)}, u32[]{:S(2)}, u32[]{:S(2)}) collective-permute-start(f32[2,2,16,16,1]{4,3,2,1,0:T(8,128)S(1)} %fusion), channel_id=1, source_target_pairs={{3,0},{0,1},{1,2},{2,3},{7,4},{4,5},{5,6},{6,7},{11,8},{8,9},{9,10... | collective-permute-start | bytes 12296 | tf_op jit(solution)/shard_map/ppermute | solution.py:13
  15.5 12.2 %all-to-all-start.1 = ((s32[1,32,8]{2,0,1:T(1,128)}), s32[1,32,8]{2,0,1:T(1,128)S(1)}, u32[]{:S(2)}, u32[]{:S(2)}) async-start(s32[1,32,8]{2,0,1:T(1,128)} %bitcast.10), calls=%async_computation.1 | async-start | bytes 32768 | tf_op jit(solution)/shard_map/all_to_all | solution.py:64
  27.7 10.0 %all-to-all-start.2 = ((f32[4,32,8]{2,0,1:T(4,128)}), f32[4,32,8]{2,0,1:T(4,128)S(1)}, u32[]{:S(2)}, u32[]{:S(2)}) async-start(f32[4,32,8]{2,0,1:T(4,128)} %copy.26), calls=%async_computation.2 | async-start | bytes 131072 | tf_op jit(solution)/shard_map/all_to_all | solution.py:63
  37.7 20.8 %copy-start = (f32[27,8,1]{0,1,2:T(8,128)S(1)}, f32[27,8,1]{0,1,2:T(8,128)}, u32[]{:S(2)}) copy-start(f32[27,8,1]{0,1,2:T(8,128)} %constant.39) | copy-start | bytes 2596
  37.7 18.4 %all-to-all-start = ((f32[4,32,8,128]{3,0,2,1:T(4,128)}), f32[4,32,8,128]{3,0,2,1:T(4,128)S(1)}, u32[]{:S(2)}, u32[]{:S(2)}) async-start(f32[4,32,8,128]{3,0,2,1:T(4,128)} %bitcast.8), calls=%async_computation | async-start | bytes 1048576 | tf_op jit(solution)/shard_map/all_to_all | solution.py:62
where the time goes:
time: 67 us; the launch traced here: 66.7 us
  waiting for transfers between devices  20.8 us (31%)
  local copies, waits for them, and re-layouts  15.5 us (23%)
  starting transfers between devices  15.3 us (23%)
  other arithmetic  10.5 us (16%)
  matrix products  3.72 us (6%)
  between operations  0.83 us (1%)
    all_to_all x1, waiting for transfers between devices, shards(): lax.all_to_all(packed, ('gx', 'gy', 'gz'), split_axis=1, concat_axis=1, t...  8.3 us
    all_to_all x1, waiting for transfers between devices, shards(): lax.all_to_all(rim_packed, ('gx', 'gy', 'gz'), split_axis=1, concat_axis=...  5.26 us
    all_to_all x1, starting transfers between devices, shards(): lax.all_to_all(slot_ids, ('gx', 'gy', 'gz'), split_axis=1, concat_axis=1,...  5.1 us
    ppermute x3, starting transfers between devices, from_behind(): return lax.ppermute(block, axis, route)  4.74 us
    all_to_all x1, waiting for transfers between devices, shards(): lax.all_to_all(slot_ids, ('gx', 'gy', 'gz'), split_axis=1, concat_axis=1,...  4.21 us
    unnamed x3, local copies, waits for them, and re-layouts  3.85 us
    dot_general x1, matrix products, shards(): jnp.einsum('oa,alz->olz', table, corners, precision=lax.Precision.HIGHEST)  3.72 us
    sort x1, other arithmetic, shards(): by_owner = jnp.argsort(owner_dev, stable=True)  3.17 us
  transfers between devices with their start and end apart: 6, of which 5 were waited for; matrix products, arithmetic and copies ran while one was open for 27% of the time, Pallas kernels for 0%

commit v1 on v0

--- a/solution.py
+++ b/solution.py
@@ -61,7 +61,15 @@
     got_lines, got_rims, got_slots = (
         lax.all_to_all(packed, ("gx", "gy", "gz"), split_axis=1, concat_axis=1, tiled=True),
         lax.all_to_all(rim_packed, ("gx", "gy", "gz"), split_axis=1, concat_axis=1, tiled=True),
-        lax.all_to_all(slot_ids, ("gx", "gy", "gz"), split_axis=1, concat_axis=1, tiled=True),
+        jnp.concatenate(
+            lax.all_to_all(
+                jnp.stack(jnp.split(slot_ids, lax.axis_size(("gx", "gy", "gz")), axis=1)),
+                ("gx", "gy", "gz"),
+                0,
+                0,
+            ),
+            axis=1,
+        ),
     )
     placing = jnp.argsort(got_slots.reshape(-1))
     current = got_lines.reshape(4, line_count, span_z)[:, placing]

time: 67 us -> 83.2 us (1.24)
  local copies, waits for them, and re-layouts: 15.5 us -> 31.3 us
    unnamed x3 -> x34, local copies, waits for them, and re-layouts: 3.85 us -> 19.7 us
    ppermute x3, waiting for transfers between devices: 3.03 us -> 5.16 us  [from_behind(): return lax.ppermute(block, axis, route)]
    all_to_all x1, waiting for transfers between devices: 4.21 us -> 2.07 us  [shards(): lax.all_to_all(jnp.stack(jnp.split(slot_ids, lax.axis_size(('gx', 'gy', '...]
  transfers between devices with their start and end apart: 6 -> 6, of which waited for: 5 -> 5; matrix products, arithmetic and copies ran while one was open for 27% -> 41% of each run, Pallas kernels for 0% -> 0%
where the time goes in v1:
time: 83.2 us; the launch traced here: 82.8 us
  local copies, waits for them, and re-layouts  31.3 us (38%)
  waiting for transfers between devices  20.8 us (25%)
  starting transfers between devices  15.7 us (19%)
  other arithmetic  10.5 us (13%)
  matrix products  3.72 us (4%)
  between operations  0.84 us (1%)
    unnamed x34, local copies, waits for them, and re-layouts  19.7 us
    all_to_all x1, waiting for transfers between devices, shards(): lax.all_to_all(packed, ('gx', 'gy', 'gz'), split_axis=1, concat_axis=1, t...  8.3 us
    all_to_all x1, waiting for transfers between devices, shards(): lax.all_to_all(rim_packed, ('gx', 'gy', 'gz'), split_axis=1, concat_axis=...  5.26 us
    ppermute x3, waiting for transfers between devices, from_behind(): return lax.ppermute(block, axis, route)  5.16 us
    all_to_all x1, starting transfers between devices, shards(): lax.all_to_all(jnp.stack(jnp.split(slot_ids, lax.axis_size(('gx', 'gy', '...  5.1 us
    ppermute x3, starting transfers between devices, from_behind(): return lax.ppermute(block, axis, route)  4.74 us
    dot_general x1, matrix products, shards(): jnp.einsum('oa,alz->olz', table, corners, precision=lax.Precision.HIGHEST)  3.72 us
    sort x1, other arithmetic, shards(): by_owner = jnp.argsort(owner_dev, stable=True)  3.17 us
  transfers between devices with their start and end apart: 6, of which 5 were waited for; matrix products, arithmetic and copies ran while one was open for 41% of the time, Pallas kernels for 0%

profile of v1, /device:TPU:0, one launch (start us, length us, event | category | flops | bytes accessed | tf_op | source)
XLA Modules:
  0.0 82.8 jit_solution(1770591275847221731)
XLA Ops:
  0.6 1.0 %exponential_multiply_fusion = f32[16,16,128]{2,1,0:T(8,128)S(1)} fusion(f32[16,16,128]{2,1,0:T(8,128)} %param.4, s32[16,16,128]{2,1,0:T(8,128)} %param.5), kind=kLoop, calls=%fused_computation.20 | loop fusion | flops 98304 | bytes 393216 | tf_op jit(solution)/shard_map/mul | solution.py:40
  1.6 3.1 %collective-permute-start = (f32[1,16,128]{2,1,0:T(8,128)S(1)}, f32[1,16,128]{2,1,0:T(8,128)S(1)}, u32[]{:S(2)}, u32[]{:S(2)}) collective-permute-start(f32[1,16,128]{2,1,0:T(8,128)S(1)} %slice.34), channel_id=1, source_target_pairs={{24,0},{0,8},{8,16},{16,24},{25,1},{1,9},{9,17},{17,25},{26,2},{2,... | collective-permute-start | bytes 24584 | tf_op jit(solution)/shard_map/ppermute | solution.py:13
  4.7 0.7 and_select_fusion
  5.4 3.2 %sort.34 = (s32[256]{0:T(256)}, s32[256]{0:T(256)S(1)}) sort(s32[256]{0:T(256)S(1)} %get-tuple-element.19, s32[256]{0:T(256)S(1)} %iota.8), dimensions={0}, to_apply=%region_0.1 | sort | flops 2048 | bytes 4096 | tf_op jit(solution)/shard_map/jit(argsort)/sort | solution.py:52
  8.6 1.9 %gather_fusion.1 = s32[256]{0:T(256)S(1)} fusion(s32[256]{0:T(256)S(1)} %get-tuple-element.18, s32[1024]{0:T(1024)S(1)} %pad_clamp_fusion.1), kind=kCustom, calls=%fused_computation.1 | custom fusion | bytes 3072 | tf_op jit(solution)/shard_map/gather | solution.py:53
  10.6 0.5 constant_dynamic-update-slice_fusion.31
  11.2 0.5 constant_dynamic-update-slice_fusion.30
  11.7 0.5 constant_dynamic-update-slice_fusion.29
  14.2 0.5 constant_dynamic-update-slice_fusion.24
  26.7 1.6 %collective-permute-start.1 = (f32[2,16,1,128]{3,2,1,0:T(1,128)S(1)}, f32[2,16,1,128]{3,2,1,0:T(1,128)S(1)}, u32[]{:S(2)}, u32[]{:S(2)}) collective-permute-start(f32[2,16,1,128]{3,2,1,0:T(1,128)S(1)} %fusion.3), channel_id=1, source_target_pairs={{4,0},{0,4},{5,1},{1,5},{6,2},{2,6},{7,3},{3,7},{12,8},{8,12},{13,... | collective-permute-start | bytes 49160 | tf_op jit(solution)/shard_map/ppermute | solution.py:13
  28.3 2.2 %collective-permute-done.1 = f32[2,16,1,128]{3,2,1,0:T(1,128)S(1)} collective-permute-done((f32[2,16,1,128]{3,2,1,0:T(1,128)S(1)}, f32[2,16,1,128]{3,2,1,0:T(1,128)S(1)}, u32[]{:S(2)}, u32[]{:S(2)}) %collective-permute-start.1) | collective-permute-done | bytes 16416 | tf_op jit(solution)/shard_map/ppermute | solution.py:13
  30.8 0.5 constant_dynamic-update-slice_fusion
  31.3 5.1 %all-to-all-start.1 = ((s32[32,1,1,8]{3,2,1,0:T(1,128)}), s32[32,1,1,8]{3,2,1,0:T(1,128)S(1)}, u32[]{:S(2)}, u32[]{:S(2)}) async-start(s32[32,1,1,8]{3,2,1,0:T(1,128)} %constant_dynamic-update-slice_fusion), calls=%async_computation.1 | async-start | bytes 32768 | tf_op jit(solution)/shard_map/all_to_all | solution.py:65
  36.4 3.0 %collective-permute-done.2 = f32[2,2,16,16,1]{4,3,2,1,0:T(8,128)S(1)} collective-permute-done((f32[2,2,16,16,1]{4,3,2,1,0:T(8,128)S(1)}, f32[2,2,16,16,1]{4,3,2,1,0:T(8,128)S(1)}, u32[]{:S(2)}, u32[]{:S(2)}) %collective-permute-start.2) | collective-permute-done | bytes 4128 | tf_op jit(solution)/shard_map/ppermute | solution.py:13
  39.8 0.7 gather_fusion.3
  40.5 0.9 %copy.109 = f32[4,32,8]{2,0,1:T(4,128)} copy(f32[4,32,8]{0,2,1:T(8,128)S(1)} %bitcast.171) | data formatting | bytes 8192 | tf_op jit(solution)/shard_map/reshape | solution.py:60
  41.4 2.1 %all-to-all-done.1 = s32[32,1,1,8]{3,2,1,0:T(1,128)S(1)} async-done(((s32[32,1,1,8]{3,2,1,0:T(1,128)}), s32[32,1,1,8]{3,2,1,0:T(1,128)S(1)}, u32[]{:S(2)}, u32[]{:S(2)}) %all-to-all-start.1) | async-done | bytes 1056 | tf_op jit(solution)/shard_map/all_to_all | solution.py:65
  43.5 2.9 %all-to-all-start.2 = ((f32[4,32,8]{2,0,1:T(4,128)}), f32[4,32,8]{2,0,1:T(4,128)S(1)}, u32[]{:S(2)}, u32[]{:S(2)}) async-start(f32[4,32,8]{2,0,1:T(4,128)} %copy.109), calls=%async_computation.2 | async-start | bytes 131072 | tf_op jit(solution)/shard_map/all_to_all | solution.py:63
  46.8 1.8 %gather_fusion = f32[256,4,128]{2,1,0:T(4,128)} fusion(f32[4,256,128]{2,0,1:T(4,128)S(1)} %copy.107, s32[1024]{0:T(1024)S(1)} %pad_clamp_fusion.1), kind=kCustom, calls=%fused_computation | custom fusion | bytes 1049600 | tf_op jit(solution)/shard_map/gather | solution.py:59
  48.6 5.3 %all-to-all-done.2 = f32[4,32,8]{2,0,1:T(4,128)S(1)} async-done(((f32[4,32,8]{2,0,1:T(4,128)}), f32[4,32,8]{2,0,1:T(4,128)S(1)}, u32[]{:S(2)}, u32[]{:S(2)}) %all-to-all-start.2) | async-done | bytes 4128 | tf_op jit(solution)/shard_map/all_to_all | solution.py:63
  53.8 2.9 %all-to-all-start = ((f32[4,32,8,128]{3,0,2,1:T(4,128)}), f32[4,32,8,128]{3,0,2,1:T(4,128)S(1)}, u32[]{:S(2)}, u32[]{:S(2)}) async-start(f32[4,32,8,128]{3,0,2,1:T(4,128)} %bitcast.8), calls=%async_computation | async-start | bytes 1048576 | tf_op jit(solution)/shard_map/all_to_all | solution.py:62
  56.7 0.5 broadcast.55
  57.3 0.7 reduce.4
  58.1 3.2 %sort.35 = (s32[256]{0:T(256)}, s32[256]{0:T(256)S(1)}) sort(s32[256]{0:T(256)S(1)} %reshape_reshape.3, s32[256]{0:T(256)S(1)} %iota.9), dimensions={0}, to_apply=%region_1.2 | sort | flops 2048 | bytes 4096 | tf_op jit(solution)/shard_map/jit(argsort)/sort | solution.py:74
  61.5 0.7 gather_fusion.4
  62.2 1.7 %copy.112 = f32[4,256,1]{2,0,1:T(4,128)S(1)} copy(f32[4,256,1]{0,1,2:T(8,128)S(1)} %bitcast.170) | data formatting | bytes 8192 | tf_op jit(solution)/shard_map/broadcast_in_dim | solution.py:77
  63.9 8.3 %all-to-all-done = f32[4,32,8,128]{3,0,2,1:T(4,128)S(1)} async-done(((f32[4,32,8,128]{3,0,2,1:T(4,128)}), f32[4,32,8,128]{3,0,2,1:T(4,128)S(1)}, u32[]{:S(2)}, u32[]{:S(2)}) %all-to-all-start) | async-done | bytes 524320 | tf_op jit(solution)/shard_map/all_to_all | solution.py:62
  72.2 1.0 %gather_fusion.2 = f32[256,4,128]{2,1,0:T(4,128)S(1)} fusion(f32[4,256,128]{2,0,1:T(4,128)S(1)} %bitcast.167, s32[1024]{0:T(1024)S(1)} %pad_clamp_fusion), kind=kCustom, calls=%fused_computation.2 | custom fusion | bytes 1049600 | tf_op jit(solution)/shard_map/gather | solution.py:75
  73.8 0.8 copy.113
  74.6 3.7 %fusion.4 = (f32[256,128]{1,0:T(8,128)S(1)}, f32[27,256,128]{2,0,1:T(8,128)S(1)}) fusion(f32[27,8,1]{0,1,2:T(8,128)S(1)} %copy-done, f32[8,256,128]{2,0,1:T(8,128)S(1)} %bitcast.163), kind=kOutput, calls=%fused_computation.98 | convolution fusion | flops 85786624 | bytes 4719456 | tf_op jit(solution)/shard_map/oa,alz->olz/dot_general | solution.py:79
  78.3 0.7 broadcast_divide_fusion
  79.0 3.8 %copy.114 = f32[27,256,128]{2,1,0:T(8,128)} copy(f32[27,256,128]{2,0,1:T(8,128)S(1)} %get-tuple-element.21) | data formatting | bytes 7077888
  (55 shorter events, 16.0 us)
Async XLA Ops:
  1.6 24.9 %collective-permute-start = (f32[1,16,128]{2,1,0:T(8,128)S(1)}, f32[1,16,128]{2,1,0:T(8,128)S(1)}, u32[]{:S(2)}, u32[]{:S(2)}) collective-permute-start(f32[1,16,128]{2,1,0:T(8,128)S(1)} %slice.34), channel_id=1, source_target_pairs={{24,0},{0,8},{8,16},{16,24},{25,1},{1,9},{9,17},{17,25},{26,2},{2,... | collective-permute-start | bytes 24584 | tf_op jit(solution)/shard_map/ppermute | solution.py:13
  26.7 3.8 %collective-permute-start.1 = (f32[2,16,1,128]{3,2,1,0:T(1,128)S(1)}, f32[2,16,1,128]{3,2,1,0:T(1,128)S(1)}, u32[]{:S(2)}, u32[]{:S(2)}) collective-permute-start(f32[2,16,1,128]{3,2,1,0:T(1,128)S(1)} %fusion.3), channel_id=1, source_target_pairs={{4,0},{0,4},{5,1},{1,5},{6,2},{2,6},{7,3},{3,7},{12,8},{8,12},{13,... | collective-permute-start | bytes 49160 | tf_op jit(solution)/shard_map/ppermute | solution.py:13
  30.7 8.7 %collective-permute-start.2 = (f32[2,2,16,16,1]{4,3,2,1,0:T(8,128)S(1)}, f32[2,2,16,16,1]{4,3,2,1,0:T(8,128)S(1)}, u32[]{:S(2)}, u32[]{:S(2)}) collective-permute-start(f32[2,2,16,16,1]{4,3,2,1,0:T(8,128)S(1)} %fusion), channel_id=1, source_target_pairs={{3,0},{0,1},{1,2},{2,3},{7,4},{4,5},{5,6},{6,7},{11,8},{8,9},{9,10... | collective-permute-start | bytes 12296 | tf_op jit(solution)/shard_map/ppermute | solution.py:13
  31.3 12.2 %all-to-all-start.1 = ((s32[32,1,1,8]{3,2,1,0:T(1,128)}), s32[32,1,1,8]{3,2,1,0:T(1,128)S(1)}, u32[]{:S(2)}, u32[]{:S(2)}) async-start(s32[32,1,1,8]{3,2,1,0:T(1,128)} %constant_dynamic-update-slice_fusion), calls=%async_computation.1 | async-start | bytes 32768 | tf_op jit(solution)/shard_map/all_to_all | solution.py:65
  43.5 10.3 %all-to-all-start.2 = ((f32[4,32,8]{2,0,1:T(4,128)}), f32[4,32,8]{2,0,1:T(4,128)S(1)}, u32[]{:S(2)}, u32[]{:S(2)}) async-start(f32[4,32,8]{2,0,1:T(4,128)} %copy.109), calls=%async_computation.2 | async-start | bytes 131072 | tf_op jit(solution)/shard_map/all_to_all | solution.py:63
  53.8 20.8 %copy-start = (f32[27,8,1]{0,1,2:T(8,128)S(1)}, f32[27,8,1]{0,1,2:T(8,128)}, u32[]{:S(2)}) copy-start(f32[27,8,1]{0,1,2:T(8,128)} %constant.39) | copy-start | bytes 2596
  53.8 18.4 %all-to-all-start = ((f32[4,32,8,128]{3,0,2,1:T(4,128)}), f32[4,32,8,128]{3,0,2,1:T(4,128)S(1)}, u32[]{:S(2)}, u32[]{:S(2)}) async-start(f32[4,32,8,128]{3,0,2,1:T(4,128)} %bitcast.8), calls=%async_computation | async-start | bytes 1048576 | tf_op jit(solution)/shard_map/all_to_all | solution.py:62
